TPU v7x, 32 devices: a whole 2x2x4 slice. The times are simulated.
32 devices in a mesh: gx: 4 (over y, x), gy: 4 (over z), gz: 2 (over core).
Axes of the slice: x: 2, y: 2, z: 4, core: 2. Of those that a mesh axis runs over, the one named last changes fastest.
Arguments:
- density: float32 [32, 256, 256], P('gx', 'gy', 'gz'), may hold values from 0.2 to 6, as said below
- momentum: float32 [3, 32, 256, 256], P(None, 'gx', 'gy', 'gz'), may hold values from -6 to 6
- energy: float32 [32, 256, 256], P('gx', 'gy', 'gz'), may hold values from 0.2 to 6, as said below
- displacement: int32 [3, 32, 256, 256], P(None, 'gx', 'gy', 'gz'), may hold values from -255 to 255
- flags: int32 [6], replicated, may hold values from 0 to 1
Outputs:
- new_density: float32 [32, 256, 256], P('gx', 'gy', 'gz')
- new_momentum: float32 [3, 32, 256, 256], P(None, 'gx', 'gy', 'gz')
- new_energy: float32 [32, 256, 256], P('gx', 'gy', 'gz')
- totals: float32 [2], replicated
Inputs may be any that keep to these rules, and one draw needn't show every extreme that they name: density is positive. energy is positive.
All inputs are finite; a program needn't handle non-finite values.
Results may differ from a plain program's by a relative error of at most 0.0003.
Values sent between devices are 32-bit elements; how exact they have to be, the bound alone decides.
A program may use at most 64 MiB of HBM per device.

v0:
```python
import jax
import jax.numpy as jnp
from jax import lax
from jax.sharding import PartitionSpec as P


def from_behind(value, axis, steps):
    count = lax.axis_size(axis)
    leading, last = (max(0, -steps), min(count, count - steps))
    return lax.ppermute(value, axis, [(source, source + steps) for source in range(leading, last)])


def padded_2(block, sides, width):
    for axis, dim in sides:
        count = lax.axis_size(axis)
        forward = [(i, i + 1) for i in range(count - 1)]
        backward = [(target, source) for source, target in forward]
        low = lax.ppermute(
            lax.slice_in_dim(block, block.shape[dim] - width, None, axis=dim), axis, forward
        )
        high = lax.ppermute(lax.slice_in_dim(block, 0, width, axis=dim), axis, backward)
        block = jnp.concatenate([low, block, high], axis=dim)
    return block


def minmod(left_diff, right_diff):
    return (
        0.5
        * (jnp.sign(left_diff) + jnp.sign(right_diff))
        * jnp.minimum(jnp.abs(left_diff), jnp.abs(right_diff))
    )


def flux_change(padded, face_rows, along):
    total_len = padded.shape[along]
    upper_cells = lax.slice_in_dim(padded, 2, total_len, axis=along)
    middle = lax.slice_in_dim(padded, 1, total_len - 1, axis=along)
    lower_cells = lax.slice_in_dim(padded, 0, total_len - 2, axis=along)
    slopes = minmod(upper_cells - middle, middle - lower_cells)
    k = total_len - 2
    low_val = lax.slice_in_dim(middle, 0, k - 1, axis=along)
    high_val = lax.slice_in_dim(middle, 1, k, axis=along)
    low_slope = lax.slice_in_dim(slopes, 0, k - 1, axis=along)
    high_slope = lax.slice_in_dim(slopes, 1, k, axis=along)
    fluxes = face_rows * jnp.where(
        face_rows > 0,
        low_val + 0.5 * (1.0 - face_rows) * low_slope,
        high_val - 0.5 * (1.0 + face_rows) * high_slope,
    )
    m = k - 1
    return lax.slice_in_dim(fluxes, 0, m - 1, axis=along) - lax.slice_in_dim(
        fluxes, 1, m, axis=along
    )


def fix_ghosts(padded, along, position, count_on):
    total_len = padded.shape[along]
    first_cell = lax.slice_in_dim(padded, 2, 3, axis=along)
    last_cell = lax.slice_in_dim(padded, total_len - 3, total_len - 2, axis=along)
    low_ghosts = jnp.where(
        position == 0,
        jnp.concatenate([first_cell, first_cell], along),
        lax.slice_in_dim(padded, 0, 2, axis=along),
    )
    high_ghosts = jnp.where(
        position == count_on - 1,
        jnp.concatenate([last_cell, last_cell], along),
        lax.slice_in_dim(padded, total_len - 2, total_len, axis=along),
    )
    return jnp.concatenate(
        [low_ghosts, lax.slice_in_dim(padded, 2, total_len - 2, axis=along), high_ghosts], along
    )


def face_edges(face_speed, comp, position, flag_open):
    n = face_speed.shape[comp]
    low_face = lax.slice_in_dim(face_speed, 0, 1, axis=comp) * jnp.where(
        position == 0, flag_open[2 * comp], 1.0
    )
    last_face = lax.slice_in_dim(face_speed, n - 1, n, axis=comp) * flag_open[2 * comp + 1]
    return (low_face, last_face)


def face_build(face_speed, comp, next_plane, position, count_on, flag_open):
    n = face_speed.shape[comp]
    low_face, last_face = face_edges(face_speed, comp, position, flag_open)
    high_face = jnp.where(
        position == count_on - 1, last_face, next_plane.astype(jnp.float32) / 256.0
    )
    face_rows = jnp.concatenate(
        [low_face, lax.slice_in_dim(face_speed, 1, n, axis=comp), high_face], comp
    )
    return face_rows[None]


def shards(density, momentum, energy, displacement, flags):
    fields = jnp.concatenate([density[None], momentum, energy[None]], 0)
    face_speed = displacement.astype(jnp.float32) / 256.0
    flag_open = flags.astype(jnp.float32)
    pos_x, pos_y, pos_z = (lax.axis_index("gx"), lax.axis_index("gy"), lax.axis_index("gz"))
    size_x, size_y, size_z = (lax.axis_size("gx"), lax.axis_size("gy"), lax.axis_size("gz"))
    cell_total = float(
        fields.shape[1] * fields.shape[2] * fields.shape[3] * size_x * size_y * size_z
    )
    next_xplane = from_behind(displacement[0, 0:1], "gx", -1)
    next_yplane = from_behind(displacement[1, :, 0:1], "gy", -1)
    next_zplane = from_behind(displacement[2, :, :, 0:1], "gz", -1)
    faces_x = face_build(face_speed[0], 0, next_xplane, pos_x, size_x, flag_open)
    faces_y = face_build(face_speed[1], 1, next_yplane, pos_y, size_y, flag_open)
    faces_z = face_build(face_speed[2], 2, next_zplane, pos_z, size_z, flag_open)
    along_x = padded_2(fields, (("gx", 1),), 2)
    along_y = padded_2(fields, (("gy", 2),), 2)
    along_z = padded_2(fields, (("gz", 3),), 2)
    updated = fields + flux_change(fix_ghosts(along_x, 1, pos_x, size_x), faces_x, 1)
    updated = updated + flux_change(fix_ghosts(along_y, 2, pos_y, size_y), faces_y, 2)
    updated = updated + flux_change(fix_ghosts(along_z, 3, pos_z, size_z), faces_z, 3)
    mass_sum, energy_sum = lax.psum((jnp.sum(updated[0]), jnp.sum(updated[4])), ("gx", "gy", "gz"))
    totals = jnp.stack([mass_sum, energy_sum]) / cell_total
    return (updated[0], updated[1:4], updated[4], totals)


def solution(mesh):
    return jax.shard_map(
        shards,
        mesh=mesh,
        in_specs=(
            P("gx", "gy", "gz"),
            P(None, "gx", "gy", "gz"),
            P("gx", "gy", "gz"),
            P(None, "gx", "gy", "gz"),
            P(),
        ),
        out_specs=(P("gx", "gy", "gz"), P(None, "gx", "gy", "gz"), P("gx", "gy", "gz"), P()),
        check_vma=False,
    )
```

profile of v0, /device:TPU:0, one launch (start us, length us, event | category | flops | bytes accessed | tf_op | source)
XLA Modules:
  0.0 120.2 jit_solution(10751196906076878649)
XLA Ops:
  0.6 1.4 %pad_maximum_fusion.15 = f32[5,8,64,128]{3,2,1,0:T(8,128)S(1)} fusion(f32[1,8,64,128]{3,2,1,0:T(8,128)} %bitcast.35, f32[3,8,64,128]{3,2,1,0:T(8,128)} %param.6, f32[1,8,64,128]{3,2,1,0:T(8,128)} %bitcast.43), kind=kLoop, calls=%fused_computation.45 | loop fusion | flops 655360 | bytes 2621440 | tf_op jit(solution)/shard_map/concatenate | solution.py:97
  2.0 1.6 %fusion.24 = (f32[5,8,64,2]{3,2,1,0:T(8,128)}, f32[5,8,64,2]{3,2,1,0:T(8,128)S(1)}) fusion(f32[5,8,64,128]{3,2,1,0:T(8,128)S(1)} %pad_maximum_fusion.15), kind=kLoop, calls=%fused_computation.91 | loop fusion | bytes 81920 | tf_op jit(solution)/shard_map/slice | solution.py:19
  3.5 2.4 %copy.143 = f32[5,8,64,2]{2,1,3,0:T(8,128)} copy(f32[5,8,64,2]{3,2,1,0:T(8,128)} %get-tuple-element.32) | data formatting | bytes 40960 | tf_op jit(solution)/shard_map/slice | solution.py:19
  6.0 3.0 %collective-permute-start.7 = (f32[5,8,64,2]{2,1,3,0:T(8,128)}, f32[5,8,64,2]{2,1,3,0:T(8,128)}, u32[]{:S(2)}, u32[]{:S(2)}) collective-permute-start(f32[5,8,64,2]{2,1,3,0:T(8,128)} %copy.143), channel_id=1, source_target_pairs={{0,1},{2,3},{4,5},{6,7},{8,9},{10,11},{12,13},{14,15},{16,17},{18,... | collective-permute-start | bytes 61448 | tf_op jit(solution)/shard_map/ppermute | solution.py:18
  9.0 1.1 copy.145
  10.0 1.3 %collective-permute-start.8 = (f32[5,8,64,2]{2,1,3,0:T(8,128)}, f32[5,8,64,2]{2,1,3,0:T(8,128)}, u32[]{:S(2)}, u32[]{:S(2)}) collective-permute-start(f32[5,8,64,2]{2,1,3,0:T(8,128)} %copy.145), channel_id=1, source_target_pairs={{1,0},{3,2},{5,4},{7,6},{9,8},{11,10},{13,12},{15,14},{17,16},{19,... | collective-permute-start | bytes 61448 | tf_op jit(solution)/shard_map/ppermute | solution.py:21
  11.4 0.1 copy.148
  11.5 0.9 copy.142
  12.4 1.3 %collective-permute-start.6 = (s32[8,64,1]{2,1,0:T(8,128)}, s32[8,64,1]{2,1,0:T(8,128)}, u32[]{:S(2)}, u32[]{:S(2)}) collective-permute-start(s32[8,64,1]{2,1,0:T(8,128)} %copy.142), channel_id=1, source_target_pairs={{1,0},{3,2},{5,4},{7,6},{9,8},{11,10},{13,12},{15,14},{17,16},{19,... | collective-permute-start | bytes 6152 | tf_op jit(solution)/shard_map/ppermute | solution.py:10
  13.7 0.6 copy.137
  14.3 4.9 %collective-permute-start.4 = (f32[5,8,2,128]{3,1,2,0:T(8,128)}, f32[5,8,2,128]{3,1,2,0:T(8,128)}, u32[]{:S(2)}, u32[]{:S(2)}) collective-permute-start(f32[5,8,2,128]{3,1,2,0:T(8,128)} %copy.137), channel_id=1, source_target_pairs={{0,2},{2,4},{4,6},{1,3},{3,5},{5,7},{8,10},{10,12},{12,14},{9,11},... | collective-permute-start | bytes 122888 | tf_op jit(solution)/shard_map/ppermute | solution.py:18
  19.2 0.6 copy.139
  19.8 1.3 %collective-permute-start.5 = (f32[5,8,2,128]{3,1,2,0:T(8,128)}, f32[5,8,2,128]{3,1,2,0:T(8,128)}, u32[]{:S(2)}, u32[]{:S(2)}) collective-permute-start(f32[5,8,2,128]{3,1,2,0:T(8,128)} %copy.139), channel_id=1, source_target_pairs={{2,0},{4,2},{6,4},{3,1},{5,3},{7,5},{10,8},{12,10},{14,12},{11,9},... | collective-permute-start | bytes 122888 | tf_op jit(solution)/shard_map/ppermute | solution.py:21
  21.1 2.0 %fusion.23 = (f32[5,8,64,1]{3,2,1,0:T(8,128)}, f32[5,8,64,1]{3,2,1,0:T(8,128)}) fusion(f32[5,8,64,128]{3,2,1,0:T(8,128)S(1)} %pad_maximum_fusion.15), kind=kLoop, calls=%fused_computation.90 | loop fusion | bytes 40960 | tf_op jit(solution)/shard_map/slice | solution.py:58
  23.1 0.1 convert_multiply_fusion
  23.2 0.0 copy-start.4
  23.2 0.7 fusion.22
  23.9 0.9 fusion.20
  24.8 0.8 fusion.19
  25.6 0.6 slice_bitcast_fusion.5
  26.3 0.7 fusion.25
  27.6 0.8 slice_bitcast_fusion.6
  28.4 0.1 slice.289
  29.9 1.3 %collective-permute-start.3 = (s32[8,1,128]{2,1,0:T(1,128)S(1)}, s32[8,1,128]{2,1,0:T(1,128)S(1)}, u32[]{:S(2)}, u32[]{:S(2)}) collective-permute-start(s32[8,1,128]{2,1,0:T(1,128)S(1)} %slice_bitcast_fusion.6), channel_id=1, source_target_pairs={{2,0},{4,2},{6,4},{3,1},{5,3},{7,5},{10,8},{12,10},{14,12},{11,9},... | collective-permute-start | bytes 12296 | tf_op jit(solution)/shard_map/ppermute | solution.py:10
  31.2 1.8 %slice_multiply_fusion.7 = (f32[8,64,1]{2,1,0:T(8,128)S(1)}, f32[8,64,1]{2,1,0:T(8,128)S(1)}) fusion(f32[8,64,128]{2,1,0:T(8,128)S(1)} %get-tuple-element.35, f32[]{:T(128)S(6)} %select_n.104, s32[8,64,1]{2,1,0:T(8,128)} %collective-permute-done.6, f32[]{:T(128)} %bitcast.15, pred[]{:T(512)S(6)} %eq.29), kind=kLoop, calls=%fused_computation.62 | loop fusion | flops 2560 | bytes 10249 | tf_op jit(solution)/shard_map/mul | solution.py:77
  33.0 0.2 broadcast_compare_fusion
  33.2 1.1 subtract_multiply_fusion
  34.4 1.7 %collective-permute-done.3 = s32[8,1,128]{2,1,0:T(1,128)S(1)} collective-permute-done((s32[8,1,128]{2,1,0:T(1,128)S(1)}, s32[8,1,128]{2,1,0:T(1,128)S(1)}, u32[]{:S(2)}, u32[]{:S(2)}) %collective-permute-start.3) | collective-permute-done | bytes 4128 | tf_op jit(solution)/shard_map/ppermute | solution.py:10
  36.1 4.1 %collective-permute-start.1 = (f32[5,2,64,128]{3,2,1,0:T(8,128)}, f32[5,2,64,128]{3,2,1,0:T(8,128)}, u32[]{:S(2)}, u32[]{:S(2)}) collective-permute-start(f32[5,2,64,128]{3,2,1,0:T(8,128)} %get-tuple-element.24), channel_id=1, source_target_pairs={{0,8},{8,16},{16,24},{1,9},{9,17},{17,25},{2,10},{10,18},{18,26},{... | collective-permute-start | bytes 983048 | tf_op jit(solution)/shard_map/ppermute | solution.py:18
  40.2 0.6 slice_multiply_fusion.11
  40.7 1.0 pad_maximum_fusion.18
  41.8 0.7 broadcast_compare_fusion.1
  42.5 1.3 %collective-permute-start.2 = (f32[5,2,64,128]{3,2,1,0:T(8,128)}, f32[5,2,64,128]{3,2,1,0:T(8,128)}, u32[]{:S(2)}, u32[]{:S(2)}) collective-permute-start(f32[5,2,64,128]{3,2,1,0:T(8,128)} %get-tuple-element.25), channel_id=1, source_target_pairs={{8,0},{16,8},{24,16},{9,1},{17,9},{25,17},{10,2},{18,10},{26,18},{... | collective-permute-start | bytes 983048 | tf_op jit(solution)/shard_map/ppermute | solution.py:21
  43.8 2.3 %copy.146 = f32[5,8,64,2]{3,2,1,0:T(8,128)} copy(f32[5,8,64,2]{2,1,3,0:T(8,128)} %collective-permute-done.8) | data formatting | bytes 40960 | tf_op jit(solution)/shard_map/ppermute | solution.py:21
  46.1 2.6 %maximum_select_fusion.1 = f32[5,8,64,2]{3,2,1,0:T(8,128)S(1)} fusion(f32[5,8,64,2]{3,2,1,0:T(8,128)} %copy.146, f32[5,8,64,1]{3,2,1,0:T(8,128)} %get-tuple-element.31, pred[]{:T(512)S(6)} %eq.29), kind=kLoop, calls=%fused_computation.47 | loop fusion | flops 10240 | bytes 51201 | tf_op jit(solution)/shard_map/jit(_where)/select_n | solution.py:65
  48.8 1.7 %pad_maximum_fusion.4 = f32[5,8,64,130]{3,2,1,0:T(8,128)} fusion(f32[5,8,64,2]{3,2,1,0:T(8,128)S(1)} %maximum_select_fusion.1, f32[1,8,64,128]{3,2,1,0:T(8,128)S(1)} %bitcast.36, f32[3,8,64,128]{3,2,1,0:T(8,128)S(1)} %copy-done, f32[1,8,64,128]{3,2,1,0:T(8,128)S(1)} %bitcast.44), kind=kLoop, calls=%fused_computation.11 | loop fusion | flops 998400 | bytes 2662400 | tf_op jit(solution)/shard_map/concatenate | solution.py:70
  50.5 0.0 collective-permute-done.7
  50.5 1.5 %collective-permute-start = (s32[1,64,128]{2,1,0:T(8,128)}, s32[1,64,128]{2,1,0:T(8,128)}, u32[]{:S(2)}, u32[]{:S(2)}) collective-permute-start(s32[1,64,128]{2,1,0:T(8,128)} %slice_bitcast_fusion.5), channel_id=1, source_target_pairs={{8,0},{16,8},{24,16},{9,1},{17,9},{25,17},{10,2},{18,10},{26,18},{... | collective-permute-start | bytes 98312 | tf_op jit(solution)/shard_map/ppermute | solution.py:10
  52.0 2.4 %copy.144 = f32[5,8,64,2]{3,2,1,0:T(8,128)} copy(f32[5,8,64,2]{2,1,3,0:T(8,128)} %collective-permute-done.7) | data formatting | bytes 40960 | tf_op jit(solution)/shard_map/ppermute | solution.py:18
  54.3 2.1 %maximum_select_fusion = f32[5,8,64,2]{3,2,1,0:T(8,128)S(1)} fusion(f32[5,8,64,2]{3,2,1,0:T(8,128)} %copy.144, f32[5,8,64,1]{3,2,1,0:T(8,128)} %get-tuple-element.30, pred[]{:T(512)S(6)} %eq.28), kind=kLoop, calls=%fused_computation.46 | loop fusion | flops 10240 | bytes 51201 | tf_op jit(solution)/shard_map/jit(_where)/select_n | solution.py:60
  56.5 3.1 %maximum_maximum_fusion = (f32[5,8,64,130]{3,2,1,0:T(8,128)S(1)}, f32[5,8,64,130]{3,2,1,0:T(8,128)S(1)}) fusion(f32[1,8,64,128]{3,2,1,0:T(8,128)S(1)} %bitcast.37, f32[3,8,64,128]{3,2,1,0:T(8,128)S(1)} %copy-done, f32[1,8,64,128]{3,2,1,0:T(8,128)S(1)} %bitcast.45, f32[5,8,64,2]{3,2,1,0:T(8,128)S(1)} %maximum_select_fusion, ...), kind=kLoop, calls=%fused_computation.10 | loop fusion | flops 6656000 | bytes 4014080 | tf_op jit(solution)/shard_map/concatenate | solution.py:70
  59.6 1.4 %fusion.2 = f32[5,8,64,129]{3,2,1,0:T(8,128)S(1)} fusion(f32[5,8,64,130]{3,2,1,0:T(8,128)S(1)} %get-tuple-element.15, f32[5,8,64,130]{3,2,1,0:T(8,128)S(1)} %copy-done.3, f32[5,8,64,130]{3,2,1,0:T(8,128)S(1)} %get-tuple-element.14, f32[8,64,129]{2,1,0:T(8,128)S(1)} %copy-done.6, f32[8,64,129]{2,1,0:T(8,128)S(1)} %copy-done.5, ...), kind=kLoop, calls=%fused_computation.3 | loop fusion | flops 1981440 | bytes 7463424 | tf_op jit(solution)/shard_map/mul | solution.py:45
  61.1 1.5 %fusion.17 = f32[1,64,128]{2,1,0:T(8,128)S(1)} fusion(f32[3,8,64,128]{3,2,1,0:T(8,128)} %copy-done.4, s32[1,64,128]{2,1,0:T(8,128)} %collective-permute-done, f32[]{:T(128)} %bitcast.5, pred[]{:T(512)S(6)} %eq.25), kind=kLoop, calls=%fused_computation.77 | loop fusion | flops 32768 | bytes 98309 | tf_op jit(solution)/shard_map/jit(_where)/select_n | solution.py:87
  62.5 0.1 pad_maximum_fusion.17
  62.7 0.0 collective-permute-done.5
  62.7 0.8 maximum_select_fusion.5
  63.5 0.1 pad_maximum_fusion.14
  63.7 0.0 collective-permute-done.4
  63.7 0.8 maximum_select_fusion.4
  64.5 0.0 copy-start.13
  64.6 1.3 %maximum_maximum_fusion.2 = (f32[5,8,66,128]{3,2,1,0:T(8,128)S(1)}, f32[5,8,66,128]{3,2,1,0:T(8,128)S(1)}) fusion(f32[1,8,64,128]{3,2,1,0:T(8,128)S(1)} %bitcast.39, f32[3,8,64,128]{3,2,1,0:T(8,128)S(1)} %copy-done, f32[1,8,64,128]{3,2,1,0:T(8,128)S(1)} %bitcast.47, f32[5,8,2,128]{3,2,1,0:T(2,128)S(1)} %maximum_select_fusion.4, ...), kind=kLoop, calls=%fused_computation.36 | loop fusion | flops 6758400 | bytes 4096000 | tf_op jit(solution)/shard_map/concatenate | solution.py:70
  65.9 0.5 fusion.6
  66.4 0.4 copy-done.12
  66.8 1.0 maximum_select_fusion.3
  67.8 0.0 copy-start.11
  67.8 0.1 pad_maximum_fusion.9
  68.0 0.8 copy-done.11
  68.8 1.2 %maximum_maximum_fusion.1 = (f32[5,10,64,128]{3,2,1,0:T(8,128)S(1)}, f32[5,10,64,128]{3,2,1,0:T(8,128)S(1)}) fusion(f32[1,8,64,128]{3,2,1,0:T(8,128)S(1)} %bitcast.41, f32[3,8,64,128]{3,2,1,0:T(8,128)S(1)} %copy-done, f32[1,8,64,128]{3,2,1,0:T(8,128)S(1)} %bitcast.49, f32[5,2,64,128]{3,2,1,0:T(8,128)S(1)} %maximum_select_fusion.2, ...), kind=kLoop, calls=%fused_computation.17 | loop fusion | flops 8192000 | bytes 5242880 | tf_op jit(solution)/shard_map/concatenate | solution.py:70
  70.0 0.6 fusion.10
  70.7 0.8 fusion.12
  71.4 1.5 %slice_reduce_fusion.1 = (f32[]{:T(128)}, f32[]{:T(128)}, f32[8,64,128]{2,1,0:T(8,128)}, f32[8,64,128]{2,1,0:T(8,128)}) fusion(f32[5,8,64,128]{3,2,1,0:T(8,128)S(1)} %fusion.12), kind=kLoop, calls=%fused_computation.68 | loop fusion | flops 131070 | bytes 1048584 | tf_op jit(solution)/shard_map/reduce_sum | solution.py:117
  72.9 0.9 slice.302
  73.9 44.5 %all-reduce = (f32[1]{0:T(128)}, f32[1]{0:T(128)}) all-reduce(f32[1]{0:T(128)} %bitcast.20, f32[1]{0:T(128)} %bitcast.19), channel_id=1, replica_groups=mesh['gx'=4,'gy'=4,'gz'=2] {'gx','gy','gz'}, use_global_device_ids=true, to_apply=%region_3.4 | all-reduce | flops 2 | bytes 16 | tf_op jit(solution)/shard_map/psum | solution.py:117
  118.4 1.8 %maximum_multiply_fusion = f32[2]{0:T(128)} fusion(f32[1]{0:T(128)} %get-tuple-element.10, f32[1]{0:T(128)} %get-tuple-element.11), kind=kLoop, calls=%fused_computation.85 | loop fusion | flops 4 | bytes 16 | tf_op jit(solution)/shard_map/div | solution.py:118
  (43 shorter events, 0.3 us)
Async XLA Ops:
  3.5 7.8 %copy-start.7 = (s32[3,8,64,128]{3,2,1,0:T(8,128)S(1)}, s32[3,8,64,128]{3,2,1,0:T(8,128)}, u32[]{:S(2)}) copy-start(s32[3,8,64,128]{3,2,1,0:T(8,128)} %param.8) | copy-start | bytes 2359300
  6.0 44.5 %collective-permute-start.7 = (f32[5,8,64,2]{2,1,3,0:T(8,128)}, f32[5,8,64,2]{2,1,3,0:T(8,128)}, u32[]{:S(2)}, u32[]{:S(2)}) collective-permute-start(f32[5,8,64,2]{2,1,3,0:T(8,128)} %copy.143), channel_id=1, source_target_pairs={{0,1},{2,3},{4,5},{6,7},{8,9},{10,11},{12,13},{14,15},{16,17},{18,... | collective-permute-start | bytes 61448 | tf_op jit(solution)/shard_map/ppermute | solution.py:18
  10.0 32.5 %collective-permute-start.8 = (f32[5,8,64,2]{2,1,3,0:T(8,128)}, f32[5,8,64,2]{2,1,3,0:T(8,128)}, u32[]{:S(2)}, u32[]{:S(2)}) collective-permute-start(f32[5,8,64,2]{2,1,3,0:T(8,128)} %copy.145), channel_id=1, source_target_pairs={{1,0},{3,2},{5,4},{7,6},{9,8},{11,10},{13,12},{15,14},{17,16},{19,... | collective-permute-start | bytes 61448 | tf_op jit(solution)/shard_map/ppermute | solution.py:21
  12.4 17.6 %collective-permute-start.6 = (s32[8,64,1]{2,1,0:T(8,128)}, s32[8,64,1]{2,1,0:T(8,128)}, u32[]{:S(2)}, u32[]{:S(2)}) collective-permute-start(s32[8,64,1]{2,1,0:T(8,128)} %copy.142), channel_id=1, source_target_pairs={{1,0},{3,2},{5,4},{7,6},{9,8},{11,10},{13,12},{15,14},{17,16},{19,... | collective-permute-start | bytes 6152 | tf_op jit(solution)/shard_map/ppermute | solution.py:10
  14.3 49.3 %collective-permute-start.4 = (f32[5,8,2,128]{3,1,2,0:T(8,128)}, f32[5,8,2,128]{3,1,2,0:T(8,128)}, u32[]{:S(2)}, u32[]{:S(2)}) collective-permute-start(f32[5,8,2,128]{3,1,2,0:T(8,128)} %copy.137), channel_id=1, source_target_pairs={{0,2},{2,4},{4,6},{1,3},{3,5},{5,7},{8,10},{10,12},{12,14},{9,11},... | collective-permute-start | bytes 122888 | tf_op jit(solution)/shard_map/ppermute | solution.py:18
  19.8 42.8 %collective-permute-start.5 = (f32[5,8,2,128]{3,1,2,0:T(8,128)}, f32[5,8,2,128]{3,1,2,0:T(8,128)}, u32[]{:S(2)}, u32[]{:S(2)}) collective-permute-start(f32[5,8,2,128]{3,1,2,0:T(8,128)} %copy.139), channel_id=1, source_target_pairs={{2,0},{4,2},{6,4},{3,1},{5,3},{7,5},{10,8},{12,10},{14,12},{11,9},... | collective-permute-start | bytes 122888 | tf_op jit(solution)/shard_map/ppermute | solution.py:21
  23.2 4.4 %copy-start.4 = (f32[3,8,64,128]{3,2,1,0:T(8,128)}, f32[3,8,64,128]{3,2,1,0:T(8,128)S(1)}, u32[]{:S(2)}) copy-start(f32[3,8,64,128]{3,2,1,0:T(8,128)S(1)} %convert_multiply_fusion) | copy-start | bytes 2359300
  23.9 2.3 %copy-start.16 = (s32[6]{0:T(128)S(1)}, s32[6]{0:T(128)}, u32[]{:S(2)}) copy-start(s32[6]{0:T(128)} %param.9) | copy-start | bytes 76
  29.9 6.1 %collective-permute-start.3 = (s32[8,1,128]{2,1,0:T(1,128)S(1)}, s32[8,1,128]{2,1,0:T(1,128)S(1)}, u32[]{:S(2)}, u32[]{:S(2)}) collective-permute-start(s32[8,1,128]{2,1,0:T(1,128)S(1)} %slice_bitcast_fusion.6), channel_id=1, source_target_pairs={{2,0},{4,2},{6,4},{3,1},{5,3},{7,5},{10,8},{12,10},{14,12},{11,9},... | collective-permute-start | bytes 12296 | tf_op jit(solution)/shard_map/ppermute | solution.py:10
  36.1 31.9 %collective-permute-start.1 = (f32[5,2,64,128]{3,2,1,0:T(8,128)}, f32[5,2,64,128]{3,2,1,0:T(8,128)}, u32[]{:S(2)}, u32[]{:S(2)}) collective-permute-start(f32[5,2,64,128]{3,2,1,0:T(8,128)} %get-tuple-element.24), channel_id=1, source_target_pairs={{0,8},{8,16},{16,24},{1,9},{9,17},{17,25},{2,10},{10,18},{18,26},{... | collective-permute-start | bytes 983048 | tf_op jit(solution)/shard_map/ppermute | solution.py:18
  42.5 23.9 %collective-permute-start.2 = (f32[5,2,64,128]{3,2,1,0:T(8,128)}, f32[5,2,64,128]{3,2,1,0:T(8,128)}, u32[]{:S(2)}, u32[]{:S(2)}) collective-permute-start(f32[5,2,64,128]{3,2,1,0:T(8,128)} %get-tuple-element.25), channel_id=1, source_target_pairs={{8,0},{16,8},{24,16},{9,1},{17,9},{25,17},{10,2},{18,10},{26,18},{... | collective-permute-start | bytes 983048 | tf_op jit(solution)/shard_map/ppermute | solution.py:21
  46.1 2.6 %copy-start = (f32[3,8,64,128]{3,2,1,0:T(8,128)S(1)}, f32[3,8,64,128]{3,2,1,0:T(8,128)}, u32[]{:S(2)}) copy-start(f32[3,8,64,128]{3,2,1,0:T(8,128)} %param.6) | copy-start | bytes 2359300
  46.1 2.6 %copy-start.1 = (f32[8,64,128]{2,1,0:T(8,128)S(1)}, f32[8,64,128]{2,1,0:T(8,128)}, u32[]{:S(2)}) copy-start(f32[8,64,128]{2,1,0:T(8,128)} %param.7) | copy-start | bytes 786436
  46.1 2.6 %copy-start.2 = (f32[8,64,128]{2,1,0:T(8,128)S(1)}, f32[8,64,128]{2,1,0:T(8,128)}, u32[]{:S(2)}) copy-start(f32[8,64,128]{2,1,0:T(8,128)} %param.5) | copy-start | bytes 786436
  50.5 10.6 %collective-permute-start = (s32[1,64,128]{2,1,0:T(8,128)}, s32[1,64,128]{2,1,0:T(8,128)}, u32[]{:S(2)}, u32[]{:S(2)}) collective-permute-start(s32[1,64,128]{2,1,0:T(8,128)} %slice_bitcast_fusion.5), channel_id=1, source_target_pairs={{8,0},{16,8},{24,16},{9,1},{17,9},{25,17},{10,2},{18,10},{26,18},{... | collective-permute-start | bytes 98312 | tf_op jit(solution)/shard_map/ppermute | solution.py:10
  56.5 3.1 %copy-start.3 = (f32[5,8,64,130]{3,2,1,0:T(8,128)S(1)}, f32[5,8,64,130]{3,2,1,0:T(8,128)}, u32[]{:S(2)}) copy-start(f32[5,8,64,130]{3,2,1,0:T(8,128)} %pad_maximum_fusion.4) | copy-start | bytes 3993604
  56.5 3.1 %copy-start.5 = (f32[8,64,129]{2,1,0:T(8,128)S(1)}, f32[8,64,129]{2,1,0:T(8,128)}, u32[]{:S(2)}) copy-start(f32[8,64,129]{2,1,0:T(8,128)} %get-tuple-element.36) | copy-start | bytes 792580
  56.5 3.1 %copy-start.6 = (f32[8,64,129]{2,1,0:T(8,128)S(1)}, f32[8,64,129]{2,1,0:T(8,128)}, u32[]{:S(2)}) copy-start(f32[8,64,129]{2,1,0:T(8,128)} %get-tuple-element.37) | copy-start | bytes 792580
  61.1 1.6 %copy-start.15 = (f32[5,8,1,128]{3,2,1,0:T(1,128)S(1)}, f32[5,8,1,128]{3,2,1,0:T(1,128)}, u32[]{:S(2)}) copy-start(f32[5,8,1,128]{3,2,1,0:T(1,128)} %get-tuple-element.29) | copy-start | bytes 61444
  62.7 1.0 copy-start.14
  64.5 1.3 %copy-start.8 = (f32[8,65,128]{2,1,0:T(8,128)S(1)}, f32[8,65,128]{2,1,0:T(8,128)}, u32[]{:S(2)}) copy-start(f32[8,65,128]{2,1,0:T(8,128)} %get-tuple-element.41) | copy-start | bytes 798724
  64.5 1.3 %copy-start.9 = (f32[8,65,128]{2,1,0:T(8,128)S(1)}, f32[8,65,128]{2,1,0:T(8,128)}, u32[]{:S(2)}) copy-start(f32[8,65,128]{2,1,0:T(8,128)} %get-tuple-element.42) | copy-start | bytes 798724
  64.5 1.3 %copy-start.10 = (f32[8,65,128]{2,1,0:T(8,128)S(1)}, f32[8,65,128]{2,1,0:T(8,128)}, u32[]{:S(2)}) copy-start(f32[8,65,128]{2,1,0:T(8,128)} %get-tuple-element.43) | copy-start | bytes 798724
  64.5 1.3 %copy-start.13 = (pred[8,65,128]{2,1,0:T(8,128)(4,1)S(1)}, pred[8,65,128]{2,1,0:T(8,128)(4,1)}, u32[]{:S(2)}) copy-start(pred[8,65,128]{2,1,0:T(8,128)(4,1)} %broadcast_compare_fusion.1) | copy-start | bytes 199684
  65.9 0.9 copy-start.12
  67.8 0.9 copy-start.11
where the time goes:
time: 121 us; the launch traced here: 120 us
  blocking collectives  44.5 us (37%)
  other arithmetic  30.2 us (25%)
  local copies, waits for them, and re-layouts  20.8 us (17%)
  starting transfers between devices  19.9 us (16%)
  between operations  3.16 us (3%)
  waiting for transfers between devices  1.73 us (1%)
    psum x1, blocking collectives, shards(): lax.psum((jnp.sum(updated[0]), jnp.sum(updated[4])), ('gx', 'gy', 'gz'))  44.5 us
    ppermute x3, starting transfers between devices, padded_2(): lax.ppermute(lax.slice_in_dim(block, block.shape[dim] - width, None, axis...  12 us
    concatenate x6, other arithmetic, fix_ghosts(): jnp.concatenate([low_ghosts, lax.slice_in_dim(padded, 2, total_len - 2, a...  7.61 us
    slice x5, local copies, waits for them, and re-layouts, padded_2(): lax.slice_in_dim(block, block.shape[dim] - width, None, axis=dim)  5.54 us
    select_n x3, other arithmetic, fix_ghosts(): jnp.where(position == count_on - 1, jnp.concatenate([last_cell, last_cell...  4.44 us
    ppermute x3, starting transfers between devices, from_behind(): lax.ppermute(value, axis, [(source, source + steps) for source in range(l...  4.03 us
    ppermute x3, starting transfers between devices, padded_2(): lax.ppermute(lax.slice_in_dim(block, 0, width, axis=dim), axis, backward)  3.84 us
    slice x3, local copies, waits for them, and re-layouts, fix_ghosts(): first_cell = lax.slice_in_dim(padded, 2, 3, axis=along)  3.47 us
  transfers between devices with their start and end apart: 9, of which 1 were waited for; matrix products, arithmetic and copies ran while one was open for 31% of the time, Pallas kernels for 0%

commit v1 on v0

--- a/solution.py
+++ b/solution.py
@@ -2,6 +2,11 @@
 import jax.numpy as jnp
 from jax import lax
 from jax.sharding import PartitionSpec as P
+
+
+def one_after_other(x, axis_one, axis_two):
+    inner = lax.psum(x, axis_one)
+    return lax.psum(inner, axis_two)
 
 
 def from_behind(value, axis, steps):
@@ -114,7 +119,9 @@
     updated = fields + flux_change(fix_ghosts(along_x, 1, pos_x, size_x), faces_x, 1)
     updated = updated + flux_change(fix_ghosts(along_y, 2, pos_y, size_y), faces_y, 2)
     updated = updated + flux_change(fix_ghosts(along_z, 3, pos_z, size_z), faces_z, 3)
-    mass_sum, energy_sum = lax.psum((jnp.sum(updated[0]), jnp.sum(updated[4])), ("gx", "gy", "gz"))
+    mass_sum, energy_sum = one_after_other(
+        (jnp.sum(updated[0]), jnp.sum(updated[4])), "gx", ("gy", "gz")
+    )
     totals = jnp.stack([mass_sum, energy_sum]) / cell_total
     return (updated[0], updated[1:4], updated[4], totals)
 

time: 121 us -> 106 us (0.88)
  blocking collectives: 44.5 us -> 29.3 us
    psum x1 -> x2, blocking collectives: 44.5 us -> 29.3 us  [the longest x1 15.9 us: one_after_other(): return lax.psum(inner, axis_two)]
  transfers between devices with their start and end apart: 9 -> 9, of which waited for: 1 -> 1; matrix products, arithmetic and copies ran while one was open for 31% -> 36% of each run, Pallas kernels for 0% -> 0%
where the time goes in v1:
time: 106 us; the launch traced here: 105 us
  other arithmetic  30 us (28%)
  blocking collectives  29.3 us (28%)
  local copies, waits for them, and re-layouts  20.7 us (20%)
  starting transfers between devices  19.9 us (19%)
  between operations  2.96 us (3%)
  waiting for transfers between devices  1.81 us (2%)
    psum x1, blocking collectives, one_after_other(): return lax.psum(inner, axis_two)  15.9 us
    psum x1, blocking collectives, one_after_other(): inner = lax.psum(x, axis_one)  13.4 us
    ppermute x3, starting transfers between devices, padded_2(): lax.ppermute(lax.slice_in_dim(block, block.shape[dim] - width, None, axis...  12 us
    concatenate x6, other arithmetic, fix_ghosts(): jnp.concatenate([low_ghosts, lax.slice_in_dim(padded, 2, total_len - 2, a...  7.62 us
    slice x5, local copies, waits for them, and re-layouts, padded_2(): lax.slice_in_dim(block, block.shape[dim] - width, None, axis=dim)  5.54 us
    select_n x3, other arithmetic, fix_ghosts(): jnp.where(position == count_on - 1, jnp.concatenate([last_cell, last_cell...  4.44 us
    ppermute x3, starting transfers between devices, from_behind(): lax.ppermute(value, axis, [(source, source + steps) for source in range(l...  4.03 us
    ppermute x3, starting transfers between devices, padded_2(): lax.ppermute(lax.slice_in_dim(block, 0, width, axis=dim), axis, backward)  3.84 us
  transfers between devices with their start and end apart: 9, of which 1 were waited for; matrix products, arithmetic and copies ran while one was open for 36% of the time, Pallas kernels for 0%

profile of v1, /device:TPU:0, one launch (start us, length us, event | category | flops | bytes accessed | tf_op | source)
XLA Modules:
  0.0 104.8 jit_solution(1482250398412368108)
XLA Ops:
  0.6 1.4 %pad_maximum_fusion.15 = f32[5,8,64,128]{3,2,1,0:T(8,128)S(1)} fusion(f32[1,8,64,128]{3,2,1,0:T(8,128)} %bitcast.35, f32[3,8,64,128]{3,2,1,0:T(8,128)} %param.6, f32[1,8,64,128]{3,2,1,0:T(8,128)} %bitcast.43), kind=kLoop, calls=%fused_computation.45 | loop fusion | flops 655360 | bytes 2621440 | tf_op jit(solution)/shard_map/concatenate | solution.py:102
  2.0 1.6 %fusion.24 = (f32[5,8,64,2]{3,2,1,0:T(8,128)}, f32[5,8,64,2]{3,2,1,0:T(8,128)S(1)}) fusion(f32[5,8,64,128]{3,2,1,0:T(8,128)S(1)} %pad_maximum_fusion.15), kind=kLoop, calls=%fused_computation.91 | loop fusion | bytes 81920 | tf_op jit(solution)/shard_map/slice | solution.py:24
  3.5 2.4 %copy.143 = f32[5,8,64,2]{2,1,3,0:T(8,128)} copy(f32[5,8,64,2]{3,2,1,0:T(8,128)} %get-tuple-element.34) | data formatting | bytes 40960 | tf_op jit(solution)/shard_map/slice | solution.py:24
  6.0 3.0 %collective-permute-start.7 = (f32[5,8,64,2]{2,1,3,0:T(8,128)}, f32[5,8,64,2]{2,1,3,0:T(8,128)}, u32[]{:S(2)}, u32[]{:S(2)}) collective-permute-start(f32[5,8,64,2]{2,1,3,0:T(8,128)} %copy.143), channel_id=1, source_target_pairs={{0,1},{2,3},{4,5},{6,7},{8,9},{10,11},{12,13},{14,15},{16,17},{18,... | collective-permute-start | bytes 61448 | tf_op jit(solution)/shard_map/ppermute | solution.py:23
  9.0 1.0 copy.145
  10.0 1.3 %collective-permute-start.8 = (f32[5,8,64,2]{2,1,3,0:T(8,128)}, f32[5,8,64,2]{2,1,3,0:T(8,128)}, u32[]{:S(2)}, u32[]{:S(2)}) collective-permute-start(f32[5,8,64,2]{2,1,3,0:T(8,128)} %copy.145), channel_id=1, source_target_pairs={{1,0},{3,2},{5,4},{7,6},{9,8},{11,10},{13,12},{15,14},{17,16},{19,... | collective-permute-start | bytes 61448 | tf_op jit(solution)/shard_map/ppermute | solution.py:26
  11.4 0.1 copy.148
  11.5 0.9 copy.142
  12.4 1.3 %collective-permute-start.6 = (s32[8,64,1]{2,1,0:T(8,128)}, s32[8,64,1]{2,1,0:T(8,128)}, u32[]{:S(2)}, u32[]{:S(2)}) collective-permute-start(s32[8,64,1]{2,1,0:T(8,128)} %copy.142), channel_id=1, source_target_pairs={{1,0},{3,2},{5,4},{7,6},{9,8},{11,10},{13,12},{15,14},{17,16},{19,... | collective-permute-start | bytes 6152 | tf_op jit(solution)/shard_map/ppermute | solution.py:15
  13.7 0.6 copy.137
  14.3 4.9 %collective-permute-start.4 = (f32[5,8,2,128]{3,1,2,0:T(8,128)}, f32[5,8,2,128]{3,1,2,0:T(8,128)}, u32[]{:S(2)}, u32[]{:S(2)}) collective-permute-start(f32[5,8,2,128]{3,1,2,0:T(8,128)} %copy.137), channel_id=1, source_target_pairs={{0,2},{2,4},{4,6},{1,3},{3,5},{5,7},{8,10},{10,12},{12,14},{9,11},... | collective-permute-start | bytes 122888 | tf_op jit(solution)/shard_map/ppermute | solution.py:23
  19.2 0.6 copy.139
  19.8 1.3 %collective-permute-start.5 = (f32[5,8,2,128]{3,1,2,0:T(8,128)}, f32[5,8,2,128]{3,1,2,0:T(8,128)}, u32[]{:S(2)}, u32[]{:S(2)}) collective-permute-start(f32[5,8,2,128]{3,1,2,0:T(8,128)} %copy.139), channel_id=1, source_target_pairs={{2,0},{4,2},{6,4},{3,1},{5,3},{7,5},{10,8},{12,10},{14,12},{11,9},... | collective-permute-start | bytes 122888 | tf_op jit(solution)/shard_map/ppermute | solution.py:26
  21.1 2.0 %fusion.23 = (f32[5,8,64,1]{3,2,1,0:T(8,128)}, f32[5,8,64,1]{3,2,1,0:T(8,128)}) fusion(f32[5,8,64,128]{3,2,1,0:T(8,128)S(1)} %pad_maximum_fusion.15), kind=kLoop, calls=%fused_computation.90 | loop fusion | bytes 40960 | tf_op jit(solution)/shard_map/slice | solution.py:63
  23.1 0.1 convert_multiply_fusion
  23.2 0.0 copy-start.4
  23.2 0.7 fusion.22
  23.9 0.9 fusion.20
  24.8 0.8 fusion.19
  25.5 0.6 slice_bitcast_fusion.5
  26.2 0.6 fusion.25
  27.6 0.8 slice_bitcast_fusion.6
  28.3 0.1 slice.289
  29.7 1.3 %collective-permute-start.3 = (s32[8,1,128]{2,1,0:T(1,128)S(1)}, s32[8,1,128]{2,1,0:T(1,128)S(1)}, u32[]{:S(2)}, u32[]{:S(2)}) collective-permute-start(s32[8,1,128]{2,1,0:T(1,128)S(1)} %slice_bitcast_fusion.6), channel_id=1, source_target_pairs={{2,0},{4,2},{6,4},{3,1},{5,3},{7,5},{10,8},{12,10},{14,12},{11,9},... | collective-permute-start | bytes 12296 | tf_op jit(solution)/shard_map/ppermute | solution.py:15
  31.0 1.7 %slice_multiply_fusion.7 = (f32[8,64,1]{2,1,0:T(8,128)S(1)}, f32[8,64,1]{2,1,0:T(8,128)S(1)}) fusion(f32[8,64,128]{2,1,0:T(8,128)S(1)} %get-tuple-element.37, f32[]{:T(128)S(6)} %select_n.104, s32[8,64,1]{2,1,0:T(8,128)} %collective-permute-done.6, f32[]{:T(128)} %bitcast.15, pred[]{:T(512)S(6)} %eq.29), kind=kLoop, calls=%fused_computation.62 | loop fusion | flops 2560 | bytes 10249 | tf_op jit(solution)/shard_map/mul | solution.py:82
  32.7 0.2 broadcast_compare_fusion
  32.9 1.1 %subtract_multiply_fusion = (f32[8,64,129]{2,1,0:T(8,128)}, f32[8,64,129]{2,1,0:T(8,128)}) fusion(f32[8,64,129]{2,1,0:T(8,128)S(1)} %get-tuple-element.15), kind=kLoop, calls=%fused_computation.51 | loop fusion | flops 264192 | bytes 792576 | tf_op jit(solution)/shard_map/mul | solution.py:52
  34.0 1.8 %collective-permute-done.3 = s32[8,1,128]{2,1,0:T(1,128)S(1)} collective-permute-done((s32[8,1,128]{2,1,0:T(1,128)S(1)}, s32[8,1,128]{2,1,0:T(1,128)S(1)}, u32[]{:S(2)}, u32[]{:S(2)}) %collective-permute-start.3) | collective-permute-done | bytes 4128 | tf_op jit(solution)/shard_map/ppermute | solution.py:15
  35.8 4.1 %collective-permute-start.1 = (f32[5,2,64,128]{3,2,1,0:T(8,128)}, f32[5,2,64,128]{3,2,1,0:T(8,128)}, u32[]{:S(2)}, u32[]{:S(2)}) collective-permute-start(f32[5,2,64,128]{3,2,1,0:T(8,128)} %get-tuple-element.26), channel_id=1, source_target_pairs={{0,8},{8,16},{16,24},{1,9},{9,17},{17,25},{2,10},{10,18},{18,26},{... | collective-permute-start | bytes 983048 | tf_op jit(solution)/shard_map/ppermute | solution.py:23
  39.9 0.6 slice_multiply_fusion.11
  40.6 1.0 %pad_maximum_fusion.18 = (f32[8,65,128]{2,1,0:T(8,128)}, f32[8,65,128]{2,1,0:T(8,128)}, f32[8,65,128]{2,1,0:T(8,128)}) fusion(f32[8,1,128]{2,1,0:T(1,128)S(1)} %get-tuple-element.47, f32[8,63,128]{2,1,0:T(8,128)S(1)} %slice.275, f32[8,1,128]{2,1,0:T(1,128)S(1)} %get-tuple-element.46), kind=kLoop, calls=%fused_computation.55 | loop fusion | flops 399360 | bytes 1064960 | tf_op jit(solution)/shard_map/concatenate | solution.py:95
  41.6 0.7 broadcast_compare_fusion.1
  42.3 1.3 %collective-permute-start.2 = (f32[5,2,64,128]{3,2,1,0:T(8,128)}, f32[5,2,64,128]{3,2,1,0:T(8,128)}, u32[]{:S(2)}, u32[]{:S(2)}) collective-permute-start(f32[5,2,64,128]{3,2,1,0:T(8,128)} %get-tuple-element.27), channel_id=1, source_target_pairs={{8,0},{16,8},{24,16},{9,1},{17,9},{25,17},{10,2},{18,10},{26,18},{... | collective-permute-start | bytes 983048 | tf_op jit(solution)/shard_map/ppermute | solution.py:26
  43.6 2.3 %copy.146 = f32[5,8,64,2]{3,2,1,0:T(8,128)} copy(f32[5,8,64,2]{2,1,3,0:T(8,128)} %collective-permute-done.8) | data formatting | bytes 40960 | tf_op jit(solution)/shard_map/ppermute | solution.py:26
  45.9 2.6 %maximum_select_fusion.1 = f32[5,8,64,2]{3,2,1,0:T(8,128)S(1)} fusion(f32[5,8,64,2]{3,2,1,0:T(8,128)} %copy.146, f32[5,8,64,1]{3,2,1,0:T(8,128)} %get-tuple-element.33, pred[]{:T(512)S(6)} %eq.29), kind=kLoop, calls=%fused_computation.47 | loop fusion | flops 10240 | bytes 51201 | tf_op jit(solution)/shard_map/jit(_where)/select_n | solution.py:70
  48.6 1.7 %pad_maximum_fusion.4 = f32[5,8,64,130]{3,2,1,0:T(8,128)} fusion(f32[5,8,64,2]{3,2,1,0:T(8,128)S(1)} %maximum_select_fusion.1, f32[1,8,64,128]{3,2,1,0:T(8,128)S(1)} %bitcast.36, f32[3,8,64,128]{3,2,1,0:T(8,128)S(1)} %copy-done, f32[1,8,64,128]{3,2,1,0:T(8,128)S(1)} %bitcast.44), kind=kLoop, calls=%fused_computation.11 | loop fusion | flops 998400 | bytes 2662400 | tf_op jit(solution)/shard_map/concatenate | solution.py:75
  50.3 1.5 %collective-permute-start = (s32[1,64,128]{2,1,0:T(8,128)}, s32[1,64,128]{2,1,0:T(8,128)}, u32[]{:S(2)}, u32[]{:S(2)}) collective-permute-start(s32[1,64,128]{2,1,0:T(8,128)} %slice_bitcast_fusion.5), channel_id=1, source_target_pairs={{8,0},{16,8},{24,16},{9,1},{17,9},{25,17},{10,2},{18,10},{26,18},{... | collective-permute-start | bytes 98312 | tf_op jit(solution)/shard_map/ppermute | solution.py:15
  51.8 2.4 %copy.144 = f32[5,8,64,2]{3,2,1,0:T(8,128)} copy(f32[5,8,64,2]{2,1,3,0:T(8,128)} %collective-permute-done.7) | data formatting | bytes 40960 | tf_op jit(solution)/shard_map/ppermute | solution.py:23
  54.2 2.1 %maximum_select_fusion = f32[5,8,64,2]{3,2,1,0:T(8,128)S(1)} fusion(f32[5,8,64,2]{3,2,1,0:T(8,128)} %copy.144, f32[5,8,64,1]{3,2,1,0:T(8,128)} %get-tuple-element.32, pred[]{:T(512)S(6)} %eq.28), kind=kLoop, calls=%fused_computation.46 | loop fusion | flops 10240 | bytes 51201 | tf_op jit(solution)/shard_map/jit(_where)/select_n | solution.py:65
  56.3 3.1 %maximum_maximum_fusion = (f32[5,8,64,130]{3,2,1,0:T(8,128)S(1)}, f32[5,8,64,130]{3,2,1,0:T(8,128)S(1)}) fusion(f32[1,8,64,128]{3,2,1,0:T(8,128)S(1)} %bitcast.37, f32[3,8,64,128]{3,2,1,0:T(8,128)S(1)} %copy-done, f32[1,8,64,128]{3,2,1,0:T(8,128)S(1)} %bitcast.45, f32[5,8,64,2]{3,2,1,0:T(8,128)S(1)} %maximum_select_fusion, ...), kind=kLoop, calls=%fused_computation.10 | loop fusion | flops 6656000 | bytes 4014080 | tf_op jit(solution)/shard_map/concatenate | solution.py:75
  59.5 1.4 %fusion.2 = f32[5,8,64,129]{3,2,1,0:T(8,128)S(1)} fusion(f32[5,8,64,130]{3,2,1,0:T(8,128)S(1)} %get-tuple-element.17, f32[5,8,64,130]{3,2,1,0:T(8,128)S(1)} %copy-done.3, f32[5,8,64,130]{3,2,1,0:T(8,128)S(1)} %get-tuple-element.16, f32[8,64,129]{2,1,0:T(8,128)S(1)} %copy-done.6, f32[8,64,129]{2,1,0:T(8,128)S(1)} %copy-done.5, ...), kind=kLoop, calls=%fused_computation.3 | loop fusion | flops 1981440 | bytes 7463424 | tf_op jit(solution)/shard_map/mul | solution.py:50
  60.9 1.4 %fusion.17 = f32[1,64,128]{2,1,0:T(8,128)S(1)} fusion(f32[3,8,64,128]{3,2,1,0:T(8,128)} %copy-done.4, s32[1,64,128]{2,1,0:T(8,128)} %collective-permute-done, f32[]{:T(128)} %bitcast.5, pred[]{:T(512)S(6)} %eq.25), kind=kLoop, calls=%fused_computation.77 | loop fusion | flops 32768 | bytes 98309 | tf_op jit(solution)/shard_map/jit(_where)/select_n | solution.py:92
  62.3 0.1 pad_maximum_fusion.17
  62.5 0.8 maximum_select_fusion.5
  63.3 0.1 pad_maximum_fusion.14
  63.5 0.8 maximum_select_fusion.4
  64.3 0.0 copy-start.13
  64.3 1.3 %maximum_maximum_fusion.2 = (f32[5,8,66,128]{3,2,1,0:T(8,128)S(1)}, f32[5,8,66,128]{3,2,1,0:T(8,128)S(1)}) fusion(f32[1,8,64,128]{3,2,1,0:T(8,128)S(1)} %bitcast.39, f32[3,8,64,128]{3,2,1,0:T(8,128)S(1)} %copy-done, f32[1,8,64,128]{3,2,1,0:T(8,128)S(1)} %bitcast.47, f32[5,8,2,128]{3,2,1,0:T(2,128)S(1)} %maximum_select_fusion.4, ...), kind=kLoop, calls=%fused_computation.36 | loop fusion | flops 6758400 | bytes 4096000 | tf_op jit(solution)/shard_map/concatenate | solution.py:75
  65.7 0.5 fusion.6
  66.2 0.0 collective-permute-done.2
  66.2 0.4 copy-done.12
  66.6 1.0 maximum_select_fusion.3
  67.6 0.0 copy-start.11
  67.6 0.1 pad_maximum_fusion.9
  67.7 0.0 collective-permute-done.1
  67.8 0.8 copy-done.11
  68.6 1.2 %maximum_maximum_fusion.1 = (f32[5,10,64,128]{3,2,1,0:T(8,128)S(1)}, f32[5,10,64,128]{3,2,1,0:T(8,128)S(1)}) fusion(f32[1,8,64,128]{3,2,1,0:T(8,128)S(1)} %bitcast.41, f32[3,8,64,128]{3,2,1,0:T(8,128)S(1)} %copy-done, f32[1,8,64,128]{3,2,1,0:T(8,128)S(1)} %bitcast.49, f32[5,2,64,128]{3,2,1,0:T(8,128)S(1)} %maximum_select_fusion.2, ...), kind=kLoop, calls=%fused_computation.17 | loop fusion | flops 8192000 | bytes 5242880 | tf_op jit(solution)/shard_map/concatenate | solution.py:75
  69.8 0.6 fusion.10
  70.4 0.8 fusion.12
  71.2 1.4 %slice_reduce_fusion.1 = (f32[]{:T(128)}, f32[]{:T(128)}, f32[8,64,128]{2,1,0:T(8,128)}, f32[8,64,128]{2,1,0:T(8,128)}) fusion(f32[5,8,64,128]{3,2,1,0:T(8,128)S(1)} %fusion.12), kind=kLoop, calls=%fused_computation.68 | loop fusion | flops 131070 | bytes 1048584 | tf_op jit(solution)/shard_map/reduce_sum | solution.py:123
  72.7 0.9 slice.302
  73.6 13.4 %all-reduce.1 = (f32[]{:T(128)}, f32[]{:T(128)}) all-reduce(f32[]{:T(128)} %get-tuple-element.9, f32[]{:T(128)} %get-tuple-element.8), channel_id=1, replica_groups=mesh['gx'=4,'gy'=4,'gz'=2] {'gx'}, use_global_device_ids=true, to_apply=%region_4.5 | all-reduce | flops 2 | bytes 16 | tf_op jit(solution)/shard_map/psum | solution.py:8
  87.0 15.9 %all-reduce = (f32[1]{0:T(128)}, f32[1]{0:T(128)}) all-reduce(f32[1]{0:T(128)} %bitcast.20, f32[1]{0:T(128)} %bitcast.19), channel_id=1, replica_groups=mesh['gx'=4,'gy'=4,'gz'=2] {'gy','gz'}, use_global_device_ids=true, to_apply=%region_5.6 | all-reduce | flops 2 | bytes 16 | tf_op jit(solution)/shard_map/psum | solution.py:9
  102.9 1.8 %maximum_multiply_fusion = f32[2]{0:T(128)} fusion(f32[1]{0:T(128)} %get-tuple-element.10, f32[1]{0:T(128)} %get-tuple-element.11), kind=kLoop, calls=%fused_computation.85 | loop fusion | flops 4 | bytes 16 | tf_op jit(solution)/shard_map/div | solution.py:125
  (44 shorter events, 0.3 us)
Async XLA Ops:
  3.5 7.8 %copy-start.7 = (s32[3,8,64,128]{3,2,1,0:T(8,128)S(1)}, s32[3,8,64,128]{3,2,1,0:T(8,128)}, u32[]{:S(2)}) copy-start(s32[3,8,64,128]{3,2,1,0:T(8,128)} %param.8) | copy-start | bytes 2359300
  6.0 44.3 %collective-permute-start.7 = (f32[5,8,64,2]{2,1,3,0:T(8,128)}, f32[5,8,64,2]{2,1,3,0:T(8,128)}, u32[]{:S(2)}, u32[]{:S(2)}) collective-permute-start(f32[5,8,64,2]{2,1,3,0:T(8,128)} %copy.143), channel_id=1, source_target_pairs={{0,1},{2,3},{4,5},{6,7},{8,9},{10,11},{12,13},{14,15},{16,17},{18,... | collective-permute-start | bytes 61448 | tf_op jit(solution)/shard_map/ppermute | solution.py:23
  10.0 32.3 %collective-permute-start.8 = (f32[5,8,64,2]{2,1,3,0:T(8,128)}, f32[5,8,64,2]{2,1,3,0:T(8,128)}, u32[]{:S(2)}, u32[]{:S(2)}) collective-permute-start(f32[5,8,64,2]{2,1,3,0:T(8,128)} %copy.145), channel_id=1, source_target_pairs={{1,0},{3,2},{5,4},{7,6},{9,8},{11,10},{13,12},{15,14},{17,16},{19,... | collective-permute-start | bytes 61448 | tf_op jit(solution)/shard_map/ppermute | solution.py:26
  12.4 17.3 %collective-permute-start.6 = (s32[8,64,1]{2,1,0:T(8,128)}, s32[8,64,1]{2,1,0:T(8,128)}, u32[]{:S(2)}, u32[]{:S(2)}) collective-permute-start(s32[8,64,1]{2,1,0:T(8,128)} %copy.142), channel_id=1, source_target_pairs={{1,0},{3,2},{5,4},{7,6},{9,8},{11,10},{13,12},{15,14},{17,16},{19,... | collective-permute-start | bytes 6152 | tf_op jit(solution)/shard_map/ppermute | solution.py:15
  14.3 49.1 %collective-permute-start.4 = (f32[5,8,2,128]{3,1,2,0:T(8,128)}, f32[5,8,2,128]{3,1,2,0:T(8,128)}, u32[]{:S(2)}, u32[]{:S(2)}) collective-permute-start(f32[5,8,2,128]{3,1,2,0:T(8,128)} %copy.137), channel_id=1, source_target_pairs={{0,2},{2,4},{4,6},{1,3},{3,5},{5,7},{8,10},{10,12},{12,14},{9,11},... | collective-permute-start | bytes 122888 | tf_op jit(solution)/shard_map/ppermute | solution.py:23
  19.8 42.6 %collective-permute-start.5 = (f32[5,8,2,128]{3,1,2,0:T(8,128)}, f32[5,8,2,128]{3,1,2,0:T(8,128)}, u32[]{:S(2)}, u32[]{:S(2)}) collective-permute-start(f32[5,8,2,128]{3,1,2,0:T(8,128)} %copy.139), channel_id=1, source_target_pairs={{2,0},{4,2},{6,4},{3,1},{5,3},{7,5},{10,8},{12,10},{14,12},{11,9},... | collective-permute-start | bytes 122888 | tf_op jit(solution)/shard_map/ppermute | solution.py:26
  23.2 4.4 %copy-start.4 = (f32[3,8,64,128]{3,2,1,0:T(8,128)}, f32[3,8,64,128]{3,2,1,0:T(8,128)S(1)}, u32[]{:S(2)}) copy-start(f32[3,8,64,128]{3,2,1,0:T(8,128)S(1)} %convert_multiply_fusion) | copy-start | bytes 2359300
  23.9 2.3 %copy-start.16 = (s32[6]{0:T(128)S(1)}, s32[6]{0:T(128)}, u32[]{:S(2)}) copy-start(s32[6]{0:T(128)} %param.9) | copy-start | bytes 76
  29.7 6.1 %collective-permute-start.3 = (s32[8,1,128]{2,1,0:T(1,128)S(1)}, s32[8,1,128]{2,1,0:T(1,128)S(1)}, u32[]{:S(2)}, u32[]{:S(2)}) collective-permute-start(s32[8,1,128]{2,1,0:T(1,128)S(1)} %slice_bitcast_fusion.6), channel_id=1, source_target_pairs={{2,0},{4,2},{6,4},{3,1},{5,3},{7,5},{10,8},{12,10},{14,12},{11,9},... | collective-permute-start | bytes 12296 | tf_op jit(solution)/shard_map/ppermute | solution.py:15
  35.8 32.0 %collective-permute-start.1 = (f32[5,2,64,128]{3,2,1,0:T(8,128)}, f32[5,2,64,128]{3,2,1,0:T(8,128)}, u32[]{:S(2)}, u32[]{:S(2)}) collective-permute-start(f32[5,2,64,128]{3,2,1,0:T(8,128)} %get-tuple-element.26), channel_id=1, source_target_pairs={{0,8},{8,16},{16,24},{1,9},{9,17},{17,25},{2,10},{10,18},{18,26},{... | collective-permute-start | bytes 983048 | tf_op jit(solution)/shard_map/ppermute | solution.py:23
  42.3 23.9 %collective-permute-start.2 = (f32[5,2,64,128]{3,2,1,0:T(8,128)}, f32[5,2,64,128]{3,2,1,0:T(8,128)}, u32[]{:S(2)}, u32[]{:S(2)}) collective-permute-start(f32[5,2,64,128]{3,2,1,0:T(8,128)} %get-tuple-element.27), channel_id=1, source_target_pairs={{8,0},{16,8},{24,16},{9,1},{17,9},{25,17},{10,2},{18,10},{26,18},{... | collective-permute-start | bytes 983048 | tf_op jit(solution)/shard_map/ppermute | solution.py:26
  45.9 2.6 %copy-start = (f32[3,8,64,128]{3,2,1,0:T(8,128)S(1)}, f32[3,8,64,128]{3,2,1,0:T(8,128)}, u32[]{:S(2)}) copy-start(f32[3,8,64,128]{3,2,1,0:T(8,128)} %param.6) | copy-start | bytes 2359300
  45.9 2.6 %copy-start.1 = (f32[8,64,128]{2,1,0:T(8,128)S(1)}, f32[8,64,128]{2,1,0:T(8,128)}, u32[]{:S(2)}) copy-start(f32[8,64,128]{2,1,0:T(8,128)} %param.7) | copy-start | bytes 786436
  45.9 2.6 %copy-start.2 = (f32[8,64,128]{2,1,0:T(8,128)S(1)}, f32[8,64,128]{2,1,0:T(8,128)}, u32[]{:S(2)}) copy-start(f32[8,64,128]{2,1,0:T(8,128)} %param.5) | copy-start | bytes 786436
  50.3 10.6 %collective-permute-start = (s32[1,64,128]{2,1,0:T(8,128)}, s32[1,64,128]{2,1,0:T(8,128)}, u32[]{:S(2)}, u32[]{:S(2)}) collective-permute-start(s32[1,64,128]{2,1,0:T(8,128)} %slice_bitcast_fusion.5), channel_id=1, source_target_pairs={{8,0},{16,8},{24,16},{9,1},{17,9},{25,17},{10,2},{18,10},{26,18},{... | collective-permute-start | bytes 98312 | tf_op jit(solution)/shard_map/ppermute | solution.py:15
  56.3 3.1 %copy-start.3 = (f32[5,8,64,130]{3,2,1,0:T(8,128)S(1)}, f32[5,8,64,130]{3,2,1,0:T(8,128)}, u32[]{:S(2)}) copy-start(f32[5,8,64,130]{3,2,1,0:T(8,128)} %pad_maximum_fusion.4) | copy-start | bytes 3993604
  56.3 3.1 %copy-start.5 = (f32[8,64,129]{2,1,0:T(8,128)S(1)}, f32[8,64,129]{2,1,0:T(8,128)}, u32[]{:S(2)}) copy-start(f32[8,64,129]{2,1,0:T(8,128)} %get-tuple-element.38) | copy-start | bytes 792580
  56.3 3.1 %copy-start.6 = (f32[8,64,129]{2,1,0:T(8,128)S(1)}, f32[8,64,129]{2,1,0:T(8,128)}, u32[]{:S(2)}) copy-start(f32[8,64,129]{2,1,0:T(8,128)} %get-tuple-element.39) | copy-start | bytes 792580
  60.9 1.6 %copy-start.15 = (f32[5,8,1,128]{3,2,1,0:T(1,128)S(1)}, f32[5,8,1,128]{3,2,1,0:T(1,128)}, u32[]{:S(2)}) copy-start(f32[5,8,1,128]{3,2,1,0:T(1,128)} %get-tuple-element.31) | copy-start | bytes 61444
  62.5 1.0 copy-start.14
  64.3 1.3 %copy-start.8 = (f32[8,65,128]{2,1,0:T(8,128)S(1)}, f32[8,65,128]{2,1,0:T(8,128)}, u32[]{:S(2)}) copy-start(f32[8,65,128]{2,1,0:T(8,128)} %get-tuple-element.43) | copy-start | bytes 798724
  64.3 1.3 %copy-start.9 = (f32[8,65,128]{2,1,0:T(8,128)S(1)}, f32[8,65,128]{2,1,0:T(8,128)}, u32[]{:S(2)}) copy-start(f32[8,65,128]{2,1,0:T(8,128)} %get-tuple-element.44) | copy-start | bytes 798724
  64.3 1.3 %copy-start.10 = (f32[8,65,128]{2,1,0:T(8,128)S(1)}, f32[8,65,128]{2,1,0:T(8,128)}, u32[]{:S(2)}) copy-start(f32[8,65,128]{2,1,0:T(8,128)} %get-tuple-element.45) | copy-start | bytes 798724
  64.3 1.3 %copy-start.13 = (pred[8,65,128]{2,1,0:T(8,128)(4,1)S(1)}, pred[8,65,128]{2,1,0:T(8,128)(4,1)}, u32[]{:S(2)}) copy-start(pred[8,65,128]{2,1,0:T(8,128)(4,1)} %broadcast_compare_fusion.1) | copy-start | bytes 199684
  65.7 0.9 copy-start.12
  67.6 0.9 copy-start.11
